TPU v7x, 32 devices: a whole 2x2x4 slice. The times are simulated.
32 devices in a mesh: lon: 8 (over y, x, core), lev: 4 (over z).
Axes of the slice: x: 2, y: 2, z: 4, core: 2. Of those that a mesh axis runs over, the one named last changes fastest.
Arguments:
- field: float32 [72, 128, 128], P('lev', 'lon'), may hold values from -6 to 6
- ens: bfloat16 [80, 72, 128, 128], P(None, 'lev', 'lon'), may hold values from -2 to 2
- sdev: float32 [72, 128, 128], P('lev', 'lon'), may hold values from 0.5 to 2
- lon_taper: bfloat16 [17], replicated, may hold values from 0 to 0.079589844
- static_taper: bfloat16 [17], replicated, may hold values from 0 to 0.079589844
- loc_vert: bfloat16 [72, 72], P('lev'), may hold values from -0.75 to 0.75
- static_vert: bfloat16 [72, 72], P('lev'), may hold values from -0.75 to 0.75
- obs_block: int32 [8192], P('lon'), may hold values from -1 to 127, as said below
- obs_value: float32 [8192], P('lon'), may hold values from -6 to 6
- obs_rinv: float32 [8192], P('lon'), may hold values from 0.25 to 4
- obs_horiz: float32 [8192, 128], P('lon'), may hold values from -0.5 to 0.5
- obs_vert: float32 [8192, 72], P('lon', 'lev'), may hold values from -0.75 to 0.75
Outputs:
- increment: float32 [72, 128, 128], P('lev', 'lon')
- adjoint_field: float32 [72, 128, 128], P('lev', 'lon')
- obs_cost: float32 [], replicated
Inputs may be any that keep to these rules, and one draw needn't show every extreme that they name: `obs_block`: each longitude sector's 1024 slots name only blocks within that sector's longitudes; live slots come first, in non-falling block order; at least half of a sector's slots are live, and some sector has all its slots live.
All inputs are finite; a program needn't handle non-finite values.
Results may differ from a plain program's by a relative error of at most 0.0041.
Values may be sent and summed in bfloat16 or wider, within the bound.
A program may use at most 128 MiB of HBM per device.

v0:
```python
import jax
import jax.numpy as jnp
from jax import lax
from jax.sharding import PartitionSpec as P

ens_weight = 0.8
static_weight = 0.5


def padded(block, sides, width):
    for axis, dim in sides:
        count = lax.axis_size(axis)
        forward = [(i, i + 1) for i in range(count - 1)]
        forward.append((count - 1, 0))
        backward = [(target, source) for source, target in forward]
        low = lax.ppermute(
            lax.slice_in_dim(block, block.shape[dim] - width, None, axis=dim), axis, forward
        )
        high = lax.ppermute(lax.slice_in_dim(block, 0, width, axis=dim), axis, backward)
        block = jnp.concatenate([low, block, high], axis=dim)
    return block


def band_matrix(taper, columns):
    width = taper.shape[0]
    extended = columns + width - 1
    offsets = jnp.arange(extended)[:, None] - jnp.arange(columns)[None, :]
    onehot = (offsets[:, :, None] == jnp.arange(width)[None, None, :]).astype(jnp.float32)
    return jnp.einsum("eid,d->ei", onehot, taper.astype(jnp.float32)).astype(jnp.bfloat16)


def body(
    field,
    ens,
    sdev,
    lon_taper,
    static_taper,
    loc_vert,
    static_vert,
    obs_block,
    obs_value,
    obs_rinv,
    obs_horiz,
    obs_vert,
):
    members, lev_rows, lon_cols, lat_rows = ens.shape
    half = lon_taper.shape[0] // 2
    zpert = (ens.astype(jnp.float32) * field[None]).astype(jnp.bfloat16)
    spart = (sdev * field).astype(jnp.bfloat16)[None]
    zwide, swide = (padded(zpert, (("lon", 2),), half), padded(spart, (("lon", 2),), half))
    zsmooth = jnp.einsum(
        "klea,ei->klia", zwide, band_matrix(lon_taper, lon_cols), preferred_element_type=jnp.float32
    ).astype(jnp.bfloat16)
    ssmooth = jnp.einsum(
        "klea,ei->klia",
        swide,
        band_matrix(static_taper, lon_cols),
        preferred_element_type=jnp.float32,
    ).astype(jnp.bfloat16)
    full_loc, full_static = (
        lax.all_gather(loc_vert, "lev", axis=0, tiled=True),
        lax.all_gather(static_vert, "lev", axis=0, tiled=True),
    )
    zcols, scols, ecols = (
        lax.all_to_all(zsmooth, "lev", split_axis=2, concat_axis=1, tiled=True),
        lax.all_to_all(ssmooth, "lev", split_axis=2, concat_axis=1, tiled=True),
        lax.all_to_all(ens, "lev", split_axis=2, concat_axis=1, tiled=True),
    )
    zvert = jnp.einsum("lm,kmia->klia", full_loc, zcols, preferred_element_type=jnp.float32)
    ens_cols = jnp.sum(ecols.astype(jnp.float32) * zvert, axis=0)[None]
    static_cols = jnp.einsum(
        "lm,kmia->klia", full_static, scols, preferred_element_type=jnp.float32
    )
    ens_back, static_back = (
        lax.all_to_all(ens_cols, "lev", split_axis=1, concat_axis=2, tiled=True),
        lax.all_to_all(static_cols, "lev", split_axis=1, concat_axis=2, tiled=True),
    )
    ens_sum = ens_back[0]
    static_sum = static_back[0]
    increment = ens_weight * ens_sum + static_weight * sdev * static_sum
    block_lon = lon_cols // 8
    block_lat = lat_rows // 16
    nblk = block_lon * block_lat
    slots = obs_block.shape[0]
    blocks = (
        increment.reshape(lev_rows, block_lon, 8, block_lat, 16)
        .transpose(0, 1, 3, 2, 4)
        .reshape(lev_rows * nblk, 128)
    )
    live = obs_block >= 0
    local_ids = obs_block - lax.axis_index("lon") * nblk
    safe = jnp.where(live, local_ids, 0)
    selector = ((jnp.arange(nblk)[:, None] == safe[None, :]) & live[None, :]).astype(jnp.float32)
    vert_rows = obs_vert.T
    projected = jnp.dot(blocks, obs_horiz.T, precision=lax.Precision.HIGHEST).reshape(
        lev_rows, nblk, slots
    )
    picked = jnp.sum(projected * selector[None], axis=1)
    partial_value = jnp.sum(picked * vert_rows, axis=0)
    hx = lax.psum(partial_value, "lev")
    miss = hx - obs_value
    dep = jnp.where(live, obs_rinv * miss, 0.0)
    obs_cost = lax.psum(0.5 * jnp.sum(dep * miss), "lon")
    weights = vert_rows * dep[None, :]
    spread = (weights[:, None, :] * selector[None]).reshape(lev_rows * nblk, slots)
    adj_blocks = jnp.dot(spread, obs_horiz, precision=lax.Precision.HIGHEST)
    adjoint_field = (
        adj_blocks.reshape(lev_rows, block_lon, block_lat, 8, 16)
        .transpose(0, 1, 3, 2, 4)
        .reshape(lev_rows, lon_cols, lat_rows)
    )
    return (increment, adjoint_field, obs_cost)


def solution(mesh):
    return jax.shard_map(
        body,
        mesh=mesh,
        in_specs=(
            P("lev", "lon", None),
            P(None, "lev", "lon", None),
            P("lev", "lon", None),
            P(),
            P(),
            P("lev", None),
            P("lev", None),
            P("lon"),
            P("lon"),
            P("lon"),
            P("lon", None),
            P("lon", "lev"),
        ),
        out_specs=(P("lev", "lon", None), P("lev", "lon", None), P()),
        check_vma=False,
    )
```

profile of v0, /device:TPU:0, one launch (start us, length us, event | category | flops | bytes accessed | tf_op | source)
XLA Modules:
  0.0 396.7 jit_solution(12835550179646047944)
XLA Ops:
  0.6 1.0 fusion.29
  1.7 0.5 collective-permute-start.2
  2.2 2.9 collective-permute-start.3
  5.2 0.5 fusion.20
  5.6 0.1 copy.93
  5.7 1.0 collective-permute-done.2
  6.8 0.1 fusion.16
  6.9 0.7 copy.83
  7.6 5.6 %all-to-all-start.3 = ((bf16[1,18,16,128]{3,1,0,2:T(8,128)(2,1)}), bf16[1,18,16,128]{3,1,0,2:T(8,128)(2,1)S(1)}, u32[]{:S(2)}, u32[]{:S(2)}) async-start(bf16[1,18,16,128]{3,1,0,2:T(8,128)(2,1)} %copy.83), calls=%async_computation.3 | async-start | bytes 196608 | tf_op jit(solution)/shard_map/all_to_all | solution.py:66
  13.2 7.5 %copy.73 = bf16[80,18,16,128]{3,0,1,2:T(8,128)(2,1)} copy(bf16[80,18,16,128]{3,2,1,0:T(8,128)(2,1)} %param.13) | data formatting | bytes 11796480 | tf_op args[1]
  20.7 5.3 %all-to-all-start = ((bf16[80,18,16,128]{3,0,1,2:T(8,128)(2,1)}), bf16[80,18,16,128]{3,0,1,2:T(8,128)(2,1)}, u32[]{:S(2)}, u32[]{:S(2)}) async-start(bf16[80,18,16,128]{3,0,1,2:T(8,128)(2,1)} %copy.73), calls=%async_computation | async-start | bytes 11796480 | tf_op jit(solution)/shard_map/all_to_all | solution.py:67
  26.0 3.8 multiply_convert_fusion
  29.8 3.1 fusion.42
  32.9 0.2 copy-done.3
  33.2 0.4 collective-permute-start
  33.6 2.2 collective-permute-start.1
  35.8 0.5 fusion.21
  36.3 0.1 copy.90
  36.4 63.5 %collective-permute-done = bf16[80,18,8,128]{3,2,1,0:T(8,128)(2,1)} collective-permute-done((bf16[80,18,8,128]{3,2,1,0:T(8,128)(2,1)}, bf16[80,18,8,128]{3,2,1,0:T(8,128)(2,1)}, u32[]{:S(2)}, u32[]{:S(2)}) %collective-permute-start) | collective-permute-done | bytes 2949152 | tf_op jit(solution)/shard_map/ppermute | solution.py:16
  99.8 5.4 %convert_bitcast_fusion.1 = bf16[80,18,16,128]{3,2,1,0:T(8,128)(2,1)S(1)} fusion(bf16[80,18,8,128]{3,2,1,0:T(8,128)(2,1)} %collective-permute-done.1, bf16[80,18,16,128]{3,2,1,0:T(8,128)(2,1)} %copy-done.3, bf16[80,18,8,128]{3,2,1,0:T(8,128)(2,1)} %collective-permute-done, bf16[1,32,16]{1,2,0:T(8,128)(2,1)S(1)} %copy.90), kind=kOutput, calls=%fused_computation.12 | convolution fusion | flops 227082240 | bytes 17695744 | tf_op jit(solution)/shard_map/klea,ei->klia/dot_general | solution.py:51
  105.3 4.8 %copy.76 = bf16[80,18,16,128]{3,0,1,2:T(8,128)(2,1)} copy(bf16[80,18,16,128]{3,2,1,0:T(8,128)(2,1)S(1)} %convert_bitcast_fusion.1) | data formatting | bytes 11796480 | tf_op jit(solution)/shard_map/convert_element_type | solution.py:53
  110.1 46.5 %all-to-all-done = bf16[80,18,16,128]{3,0,1,2:T(8,128)(2,1)} async-done(((bf16[80,18,16,128]{3,0,1,2:T(8,128)(2,1)}), bf16[80,18,16,128]{3,0,1,2:T(8,128)(2,1)}, u32[]{:S(2)}, u32[]{:S(2)}) %all-to-all-start) | async-done | bytes 5898272 | tf_op jit(solution)/shard_map/all_to_all | solution.py:67
  156.6 5.2 %all-to-all-start.1 = ((bf16[80,18,16,128]{3,0,1,2:T(8,128)(2,1)}), bf16[80,18,16,128]{3,0,1,2:T(8,128)(2,1)}, u32[]{:S(2)}, u32[]{:S(2)}) async-start(bf16[80,18,16,128]{3,0,1,2:T(8,128)(2,1)} %copy.76), calls=%async_computation.1 | async-start | bytes 11796480 | tf_op jit(solution)/shard_map/all_to_all | solution.py:65
  161.8 135.0 %all-gather = bf16[4,18,72]{2,1,0:T(8,128)(2,1)S(1)} all-gather(bf16[1,18,72]{2,1,0:T(8,128)(2,1)S(1)} %bitcast.112), channel_id=1, replica_groups=mesh['lon'=8,'lev'=4] {'lev'}, dimensions={0}, use_global_device_ids=true | all-gather | bytes 12960 | tf_op jit(solution)/shard_map/all_gather | solution.py:61
  296.9 13.3 %all-gather.1 = bf16[4,18,72]{2,1,0:T(8,128)(2,1)S(1)} all-gather(bf16[1,18,72]{2,1,0:T(8,128)(2,1)S(1)} %bitcast.113), channel_id=1, replica_groups=mesh['lon'=8,'lev'=4] {'lev'}, dimensions={0}, use_global_device_ids=true | all-gather | bytes 12960 | tf_op jit(solution)/shard_map/all_gather | solution.py:62
  310.2 1.0 copy.89
  311.3 0.1 and_convert_fusion
  311.4 0.2 convolution_bitcast_fusion.1
  311.5 0.7 copy.86
  312.2 4.3 %copy.74 = bf16[80,18,16,128]{3,0,2,1:T(8,128)(2,1)S(1)} copy(bf16[80,18,16,128]{3,0,1,2:T(8,128)(2,1)} %all-to-all-done) | data formatting | bytes 11796480 | tf_op jit(solution)/shard_map/all_to_all | solution.py:67
  316.5 6.0 %convert_bitcast_fusion = f32[80,4,18,4,128]{4,0,3,1,2:T(8,128)} fusion(bf16[80,18,4,4,128]{4,0,3,2,1:T(8,128)(2,1)S(1)} %bitcast.102), kind=kLoop, calls=%fused_computation.6 | loop fusion | flops 2949120 | bytes 17694720 | tf_op jit(solution)/shard_map/convert_element_type | solution.py:70
  322.5 10.2 %copy.75 = f32[80,4,18,4,128]{4,0,3,2,1:T(8,128)} copy(f32[80,4,18,4,128]{4,0,3,1,2:T(8,128)} %convert_bitcast_fusion) | data formatting | bytes 23592960 | tf_op jit(solution)/shard_map/convert_element_type | solution.py:70
  332.7 3.9 all-to-all-start.4
  336.5 4.5 %copy.78 = bf16[80,4,18,4,128]{4,0,3,2,1:T(8,128)(2,1)S(1)} copy(bf16[80,4,18,4,128]{4,0,2,3,1:T(8,128)(2,1)} %bitcast.10) | data formatting | bytes 11796480 | tf_op jit(solution)/shard_map/all_to_all | solution.py:65
  341.0 1.6 copy-done.2
  342.6 10.5 %fusion.6 = f32[72,4,128]{2,0,1:T(8,128)S(1)} fusion(f32[80,72,4,128]{3,0,2,1:T(8,128)S(1)} %bitcast.100, bf16[80,72,4,128]{3,0,2,1:T(8,128)(2,1)S(1)} %bitcast.101, bf16[72,72,1,1]{1,0,2,3:T(8,128)(2,1)S(1)} %reshape.131), kind=kOutput, calls=%fused_computation.8 | convolution fusion | flops 430534656 | bytes 17852544 | tf_op jit(solution)/shard_map/lm,kmia->klia/dot_general | solution.py:69
  353.1 0.7 copy.81
  353.8 5.1 %all-to-all-start.2 = ((f32[1,72,4,128]{3,2,0,1:T(4,128)}), f32[1,72,4,128]{3,2,0,1:T(4,128)S(1)}, u32[]{:S(2)}, u32[]{:S(2)}) async-start(f32[1,72,4,128]{3,2,0,1:T(4,128)} %copy.81), calls=%async_computation.2 | async-start | bytes 294912 | tf_op jit(solution)/shard_map/all_to_all | solution.py:75
  359.0 5.9 %all-to-all-done.2 = f32[1,72,4,128]{3,2,0,1:T(4,128)S(1)} async-done(((f32[1,72,4,128]{3,2,0,1:T(4,128)}), f32[1,72,4,128]{3,2,0,1:T(4,128)S(1)}, u32[]{:S(2)}, u32[]{:S(2)}) %all-to-all-start.2) | async-done | bytes 147488 | tf_op jit(solution)/shard_map/all_to_all | solution.py:75
  365.0 0.3 reshape.120
  365.4 0.2 copy.88
  365.6 0.3 dot_general.39
  366.0 1.2 fusion.13
  367.2 10.0 %psum.14 = f32[1024]{0:T(1024)S(1)} all-reduce(f32[1024]{0:T(1024)S(1)} %fusion.28), channel_id=1, replica_groups=mesh['lon'=8,'lev'=4] {'lev'}, use_global_device_ids=true, to_apply=%region_3.4 | all-reduce | flops 1024 | bytes 8192 | tf_op jit(solution)/shard_map/psum | solution.py:100
  377.2 0.6 multiply_reduce_fusion
  378.5 4.9 %convolution_bitcast_fusion = f32[18,2,8,8,16]{4,3,2,1,0:T(8,128)S(1)} fusion(f32[8,16,1024,1,1]{2,1,0,4,3:T(8,128)} %bitcast.109, f32[2,8,1024]{2,1,0:T(8,128)S(1)} %and_convert_fusion, f32[18,1024]{1,0:T(8,128)S(1)} %bitcast_multiply_fusion.1), kind=kOutput, calls=%fused_computation.13 | convolution fusion | flops 453279744 | bytes 811008 | tf_op jit(solution)/shard_map/dot_general | solution.py:106
  383.4 1.0 reshape.121
  384.4 12.3 %psum.15 = f32[]{:T(128)} all-reduce(f32[]{:T(128)S(6)} %mul.109), channel_id=1, replica_groups=mesh['lon'=8,'lev'=4] {'lon'}, use_global_device_ids=true, to_apply=%region_5.6 | all-reduce | flops 1 | bytes 8 | tf_op jit(solution)/shard_map/psum | solution.py:103
  (47 shorter events, 0.4 us)
Async XLA Ops:
  0.6 4.5 %copy-start = (bf16[17]{0:T(256)(128)(2,1)S(1)}, bf16[17]{0:T(256)(128)(2,1)}, u32[]{:S(2)}) copy-start(bf16[17]{0:T(256)(128)(2,1)} %param.16) | copy-start | bytes 106
  1.7 5.1 %collective-permute-start.2 = (bf16[1,18,8,128]{3,2,1,0:T(8,128)(2,1)S(1)}, bf16[1,18,8,128]{3,2,1,0:T(8,128)(2,1)S(1)}, u32[]{:S(2)}, u32[]{:S(2)}) collective-permute-start(bf16[1,18,8,128]{3,2,1,0:T(8,128)(2,1)S(1)} %get-tuple-element.9), channel_id=1, source_target_pairs={{0,4},{4,8},{8,12},{12,16},{16,20},{20,24},{24,28},{28,0},{1,5},{5... | collective-permute-start | bytes 110600 | tf_op jit(solution)/shard_map/ppermute | solution.py:16
  2.2 4.6 %collective-permute-start.3 = (bf16[1,18,8,128]{3,2,1,0:T(8,128)(2,1)S(1)}, bf16[1,18,8,128]{3,2,1,0:T(8,128)(2,1)S(1)}, u32[]{:S(2)}, u32[]{:S(2)}) collective-permute-start(bf16[1,18,8,128]{3,2,1,0:T(8,128)(2,1)S(1)} %get-tuple-element.10), channel_id=1, source_target_pairs={{4,0},{8,4},{12,8},{16,12},{20,16},{24,20},{28,24},{0,28},{5,1},{9... | collective-permute-start | bytes 110600 | tf_op jit(solution)/shard_map/ppermute | solution.py:19
  7.6 13.1 %all-to-all-start.3 = ((bf16[1,18,16,128]{3,1,0,2:T(8,128)(2,1)}), bf16[1,18,16,128]{3,1,0,2:T(8,128)(2,1)S(1)}, u32[]{:S(2)}, u32[]{:S(2)}) async-start(bf16[1,18,16,128]{3,1,0,2:T(8,128)(2,1)} %copy.83), calls=%async_computation.3 | async-start | bytes 196608 | tf_op jit(solution)/shard_map/all_to_all | solution.py:66
  20.7 5.3 %copy-start.7 = (f32[18,16,128]{2,1,0:T(8,128)S(1)}, f32[18,16,128]{2,1,0:T(8,128)}, u32[]{:S(2)}) copy-start(f32[18,16,128]{2,1,0:T(8,128)} %param.12) | copy-start | bytes 442372
  20.7 135.9 %all-to-all-start = ((bf16[80,18,16,128]{3,0,1,2:T(8,128)(2,1)}), bf16[80,18,16,128]{3,0,1,2:T(8,128)(2,1)}, u32[]{:S(2)}, u32[]{:S(2)}) async-start(bf16[80,18,16,128]{3,0,1,2:T(8,128)(2,1)} %copy.73), calls=%async_computation | async-start | bytes 11796480 | tf_op jit(solution)/shard_map/all_to_all | solution.py:67
  29.8 3.4 copy-start.3
  29.8 6.0 %copy-start.14 = (bf16[17]{0:T(256)(128)(2,1)S(1)}, bf16[17]{0:T(256)(128)(2,1)}, u32[]{:S(2)}) copy-start(bf16[17]{0:T(256)(128)(2,1)} %param.15) | copy-start | bytes 106
  33.2 66.7 %collective-permute-start = (bf16[80,18,8,128]{3,2,1,0:T(8,128)(2,1)}, bf16[80,18,8,128]{3,2,1,0:T(8,128)(2,1)}, u32[]{:S(2)}, u32[]{:S(2)}) collective-permute-start(bf16[80,18,8,128]{3,2,1,0:T(8,128)(2,1)} %get-tuple-element.7), channel_id=1, source_target_pairs={{0,4},{4,8},{8,12},{12,16},{16,20},{20,24},{24,28},{28,0},{1,5},{5... | collective-permute-start | bytes 8847368 | tf_op jit(solution)/shard_map/ppermute | solution.py:16
  33.6 66.2 %collective-permute-start.1 = (bf16[80,18,8,128]{3,2,1,0:T(8,128)(2,1)S(1)}, bf16[80,18,8,128]{3,2,1,0:T(8,128)(2,1)}, u32[]{:S(2)}, u32[]{:S(2)}) collective-permute-start(bf16[80,18,8,128]{3,2,1,0:T(8,128)(2,1)S(1)} %get-tuple-element.8), channel_id=1, source_target_pairs={{4,0},{8,4},{12,8},{16,12},{20,16},{24,20},{28,24},{0,28},{5,1},{9... | collective-permute-start | bytes 8847368 | tf_op jit(solution)/shard_map/ppermute | solution.py:19
  110.1 51.7 %copy-start.9 = (bf16[18,72]{1,0:T(8,128)(2,1)S(1)}, bf16[18,72]{1,0:T(8,128)(2,1)}, u32[]{:S(2)}) copy-start(bf16[18,72]{1,0:T(8,128)(2,1)} %param.17) | copy-start | bytes 7780
  110.1 186.8 %copy-start.10 = (bf16[18,72]{1,0:T(8,128)(2,1)S(1)}, bf16[18,72]{1,0:T(8,128)(2,1)}, u32[]{:S(2)}) copy-start(bf16[18,72]{1,0:T(8,128)(2,1)} %param.18) | copy-start | bytes 7780
  110.1 200.2 %copy-start.4 = (f32[1024,128]{1,0:T(8,128)S(1)}, f32[1024,128]{1,0:T(8,128)}, u32[]{:S(2)}) copy-start(f32[1024,128]{1,0:T(8,128)} %param.22) | copy-start | bytes 1572868
  110.1 201.2 %copy-start.11 = (s32[1024]{0:T(1024)S(1)}, s32[1024]{0:T(1024)}, u32[]{:S(2)}) copy-start(s32[1024]{0:T(1024)} %param.19) | copy-start | bytes 12292
  156.6 176.1 %all-to-all-start.1 = ((bf16[80,18,16,128]{3,0,1,2:T(8,128)(2,1)}), bf16[80,18,16,128]{3,0,1,2:T(8,128)(2,1)}, u32[]{:S(2)}, u32[]{:S(2)}) async-start(bf16[80,18,16,128]{3,0,1,2:T(8,128)(2,1)} %copy.76), calls=%async_computation.1 | async-start | bytes 11796480 | tf_op jit(solution)/shard_map/all_to_all | solution.py:65
  332.7 21.2 %all-to-all-start.4 = ((f32[1,72,4,128]{3,2,0,1:T(4,128)}), f32[1,72,4,128]{3,2,0,1:T(4,128)S(1)}, u32[]{:S(2)}, u32[]{:S(2)}) async-start(f32[1,72,4,128]{3,2,0,1:T(4,128)} %copy.86), calls=%async_computation.4 | async-start | bytes 294912 | tf_op jit(solution)/shard_map/all_to_all | solution.py:76
  336.5 6.1 %copy-start.2 = (f32[80,4,18,4,128]{4,0,3,2,1:T(8,128)S(1)}, f32[80,4,18,4,128]{4,0,3,2,1:T(8,128)}, u32[]{:S(2)}) copy-start(f32[80,4,18,4,128]{4,0,3,2,1:T(8,128)} %copy.75) | copy-start | bytes 35389444
  342.6 22.4 %copy-start.5 = (f32[18,16,128]{2,1,0:T(8,128)S(1)}, f32[18,16,128]{2,1,0:T(8,128)}, u32[]{:S(2)}) copy-start(f32[18,16,128]{2,1,0:T(8,128)} %param.14) | copy-start | bytes 442372
  353.1 14.1 %copy-start.8 = (f32[1024,18]{0,1:T(8,128)S(1)}, f32[1024,18]{0,1:T(8,128)}, u32[]{:S(2)}) copy-start(f32[1024,18]{0,1:T(8,128)} %param.23) | copy-start | bytes 221188
  353.1 24.1 %copy-start.12 = (f32[1024]{0:T(1024)S(1)}, f32[1024]{0:T(1024)}, u32[]{:S(2)}) copy-start(f32[1024]{0:T(1024)} %param.21) | copy-start | bytes 12292
  353.1 24.1 %copy-start.13 = (f32[1024]{0:T(1024)S(1)}, f32[1024]{0:T(1024)}, u32[]{:S(2)}) copy-start(f32[1024]{0:T(1024)} %param.20) | copy-start | bytes 12292
  353.8 11.1 %all-to-all-start.2 = ((f32[1,72,4,128]{3,2,0,1:T(4,128)}), f32[1,72,4,128]{3,2,0,1:T(4,128)S(1)}, u32[]{:S(2)}, u32[]{:S(2)}) async-start(f32[1,72,4,128]{3,2,0,1:T(4,128)} %copy.81), calls=%async_computation.2 | async-start | bytes 294912 | tf_op jit(solution)/shard_map/all_to_all | solution.py:75
  365.0 31.7 %copy-start.1 = (bf16[17]{0:T(256)(128)(2,1)S(1)}, bf16[17]{0:T(256)(128)(2,1)}, u32[]{:S(2)}) copy-start(bf16[17]{0:T(256)(128)(2,1)} %param.16) | copy-start | bytes 106
  365.0 31.7 %copy-start.6 = (f32[18,16,128]{2,1,0:T(8,128)}, f32[18,16,128]{2,1,0:T(8,128)S(1)}, u32[]{:S(2)}) copy-start(f32[18,16,128]{2,1,0:T(8,128)S(1)} %multiply_add_fusion) | copy-start | bytes 442372
where the time goes:
time: 398 us; the launch traced here: 397 us
  blocking collectives  171 us (43%)
  waiting for transfers between devices  117 us (29%)
  local copies, waits for them, and re-layouts  41.5 us (10%)
  starting transfers between devices  31.1 us (8%)
  matrix products  23.3 us (6%)
  other arithmetic  11.6 us (3%)
    all_gather x1, blocking collectives, body(): lax.all_gather(loc_vert, 'lev', axis=0, tiled=True)  135 us
    ppermute x2, waiting for transfers between devices, padded(): lax.ppermute(lax.slice_in_dim(block, block.shape[dim] - width, None, axis...  64.5 us
    all_to_all x1, waiting for transfers between devices, body(): lax.all_to_all(ens, 'lev', split_axis=2, concat_axis=1, tiled=True)  46.5 us
    all_gather x1, blocking collectives, body(): lax.all_gather(static_vert, 'lev', axis=0, tiled=True)  13.3 us
    psum x1, blocking collectives, body(): obs_cost = lax.psum(0.5 * jnp.sum(dep * miss), 'lon')  12.3 us
    unnamed x34, local copies, waits for them, and re-layouts  10.5 us
    dot_general x1, matrix products, body(): jnp.einsum('lm,kmia->klia', full_loc, zcols, preferred_element_type=jnp.f...  10.5 us
    convert_element_type x1, local copies, waits for them, and re-layouts, body(): ens_cols = jnp.sum(ecols.astype(jnp.float32) * zvert, axis=0)[None]  10.2 us
  transfers between devices with their start and end apart: 9, of which 5 were waited for; matrix products, arithmetic and copies ran while one was open for 16% of the time, Pallas kernels for 0%

commit v1 on v0

v1 whole, which is shorter than its diff:
```python
import functools

import jax
import jax.numpy as jnp
from jax import lax
from jax.experimental import pallas as pl
from jax.experimental.pallas import tpu as pltpu
from jax.sharding import PartitionSpec as P

ens_weight = 0.8
static_weight = 0.5
MESH = pl.DeviceIdType.MESH
F32 = jnp.float32
BF16 = jnp.bfloat16


def band_rows(taper, columns, lanes):
    width = taper.shape[0]
    offsets = jnp.arange(lanes)[None, :] - jnp.arange(columns)[:, None]
    onehot = (offsets[:, :, None] == jnp.arange(width)[None, None, :]).astype(F32)
    return jnp.sum(onehot * taper.astype(F32)[None, None, :], axis=2).astype(BF16)


def vert_rows(matrix, columns, lanes):
    rows, width = matrix.shape
    wide = jnp.pad(matrix, ((0, 0), (0, lanes - width)))
    return jnp.broadcast_to(wide[:, None, :], (rows, columns, lanes)).reshape(rows * columns, lanes)


def main_kernel(
    dims,
    ens,
    field,
    sdev,
    spart,
    lrep,
    srep,
    bands,
    out,
    ebuf,
    zbuf,
    hsend,
    fbuf,
    zs,
    ssend,
    lg,
    w,
    ws,
    pick,
    tband,
    acc,
    accb,
    rbuf,
    own_sem,
    ens_send,
    ens_recv,
    halo_send,
    halo_recv,
    small_send,
    small_recv,
    back_send,
    back_recv,
):
    nlev, nlon, levs, cols, half, pairs = dims
    rows = levs * cols
    full = nlev * rows
    edge = nlev * levs * half
    wide = full + 2 * edge
    me = lax.axis_index("lev")
    lon = lax.axis_index("lon")
    right, left = lax.rem(lon + 1, nlon), lax.rem(lon + nlon - 1, nlon)
    peers = [lax.rem(me + off, nlev) for off in range(1, nlev)]
    sources = [lax.rem(me + nlev - off, nlev) for off in range(1, nlev)]

    def slot(rank):
        return pl.ds(pl.multiple_of(rank * rows, 16), rows)

    own_copy = pltpu.make_async_copy(
        ens.at[pl.ds(me * 2 * pairs, 2 * pairs)], ebuf.at[:, slot(me)], own_sem
    )
    own_copy.start()

    barrier = pltpu.get_barrier_semaphore()
    for peer in peers:
        pl.semaphore_signal(barrier, inc=1, device_id={"lev": peer}, device_id_type=MESH)
    for peer in (left, right):
        pl.semaphore_signal(barrier, inc=1, device_id={"lon": peer}, device_id_type=MESH)
    pl.semaphore_wait(barrier, nlev + 1)

    def small(which, off, peer, rank):
        src, dst = ((lrep, lg), (field, fbuf), (spart, zs))[which]
        return pltpu.make_async_remote_copy(
            src_ref=src,
            dst_ref=dst.at[slot(rank)],
            send_sem=small_send.at[which, off],
            recv_sem=small_recv.at[which, off],
            device_id={"lev": peer},
            device_id_type=MESH,
        )

    def ens_copy(off, peer, rank, c):
        return pltpu.make_async_remote_copy(
            src_ref=ens.at[pl.ds(peer * 2 * pairs + 2 * c, 2)],
            dst_ref=ebuf.at[pl.ds(2 * c, 2), slot(rank)],
            send_sem=ens_send.at[off, c],
            recv_sem=ens_recv.at[off, c],
            device_id={"lev": peer},
            device_id_type=MESH,
        )

    def halo_copy(side, c):
        return pltpu.make_async_remote_copy(
            src_ref=hsend.at[side, c],
            dst_ref=zbuf.at[c, pl.ds(full + side * edge, edge)],
            send_sem=halo_send.at[side, c],
            recv_sem=halo_recv.at[side, c],
            device_id={"lon": (right, left)[side]},
            device_id_type=MESH,
        )

    def static_halo(side):
        return pltpu.make_async_remote_copy(
            src_ref=ssend.at[side],
            dst_ref=zs.at[pl.ds(full + side * edge, edge)],
            send_sem=halo_send.at[side, pairs],
            recv_sem=halo_recv.at[side, pairs],
            device_id={"lon": (right, left)[side]},
            device_id_type=MESH,
        )

    def back_copy(off, peer):
        return pltpu.make_async_remote_copy(
            src_ref=accb.at[slot(peer)],
            dst_ref=rbuf.at[off],
            send_sem=back_send.at[off],
            recv_sem=back_recv.at[off],
            device_id={"lev": peer},
            device_id_type=MESH,
        )

    for which in range(3):
        for off, peer in enumerate(peers):
            small(which, off, peer, me).start()

    def send_chunk(c, carry):
        for off, peer in enumerate(peers):
            ens_copy(off, peer, me, c).start()
        return carry

    lax.fori_loop(0, pairs, send_chunk, 0)

    lg[slot(me)] = lrep[...]
    fbuf[slot(me)] = field[...]
    zs[slot(me)] = spart[...]
    acc[...] = jnp.zeros_like(acc)

    lanes = lrep.shape[1]
    col = lax.broadcasted_iota(jnp.int32, (lanes, wide), 1)
    row = lax.broadcasted_iota(jnp.int32, (lanes, wide), 0)
    inner = col < full
    low = col < full + edge
    tail = jnp.where(low, col - full, col - full - edge)
    level = jnp.where(inner, col // cols, tail // half)
    place = jnp.where(
        inner, half + col % cols, jnp.where(low, tail % half, half + cols + tail % half)
    )
    pick[...] = jnp.where(row == level, 1.0, 0.0).astype(BF16)
    spots = jnp.where(row == place, 1.0, 0.0).astype(BF16)
    tband[...] = jnp.dot(bands[...], spots, preferred_element_type=F32)

    step = 6 * cols if (levs % 6) == 0 else cols

    def expand(src, dst, which, q):
        at = pl.ds(pl.multiple_of(q * step, 16), step)
        spread = jnp.dot(src[at], pick[...], preferred_element_type=F32)
        band = tband[which * cols : (which + 1) * cols]
        product = spread.reshape(step // cols, cols, wide) * band[None]
        dst[at] = product.reshape(step, wide).astype(BF16)

    def expand_static(q, carry):
        expand(srep, ws, 1, q)
        return carry

    lax.fori_loop(0, rows // step, expand_static, 0)

    for which in (0,):
        for off, rank in enumerate(sources):
            small(which, off, peers[off], rank).wait_recv()

    def expand_loc(q, carry):
        expand(lg, w, 0, q)
        return carry

    lax.fori_loop(0, full // step, expand_loc, 0)

    for which in (1, 2):
        for off, rank in enumerate(sources):
            small(which, off, peers[off], rank).wait_recv()

    def edges(values):
        split = values.reshape(nlev * levs, cols, values.shape[1])
        to_right = split[:, cols - half :].reshape(edge, values.shape[1]).astype(BF16)
        to_left = split[:, :half].reshape(edge, values.shape[1]).astype(BF16)
        return to_right, to_left

    ssend[0], ssend[1] = edges(zs[:full].astype(F32))
    own_copy.wait()
    for side in range(2):
        static_halo(side).start()

    tile = full // 3 if full % 48 == 0 else full

    def chunk(c, carry):
        @pl.when(c < pairs)
        def _():
            for off, rank in enumerate(sources):
                ens_copy(off, peers[off], rank, c).wait_recv()
            for h in range(2):
                at = slice(h * 128, (h + 1) * 128)
                product = ebuf[2 * c + h].astype(F32) * fbuf[...]
                hsend[0, c, :, at], hsend[1, c, :, at] = edges(product)
                zbuf[c, :full, at] = product.astype(BF16)
            for side in range(2):
                halo_copy(side, c).start()

        @pl.when(c >= 1)
        def _():
            d = c - 1
            for side in range(2):
                halo_copy(side, d).wait_recv()

            def piece(q, inner_carry):
                at = pl.ds(pl.multiple_of(q * tile, 16), tile)
                zv = jnp.dot(w[at], zbuf[d], preferred_element_type=F32)
                acc[at] += (
                    ebuf[2 * d, at].astype(F32) * zv[:, :128]
                    + ebuf[2 * d + 1, at].astype(F32) * zv[:, 128:]
                )
                return inner_carry

            lax.fori_loop(0, full // tile, piece, 0)

        return carry

    lax.fori_loop(0, pairs + 1, chunk, 0)

    accb[...] = acc[...].astype(BF16)
    for side in range(2):
        static_halo(side).wait_recv()
    static = jnp.dot(ws[...], zs[...], preferred_element_type=F32)
    base = static_weight * sdev[...] * static
    out[...] = base
    for off, peer in enumerate(peers):
        back_copy(off, peer).start()
    total = acc[slot(me)]
    for off, peer in enumerate(peers):
        back_copy(off, peer).wait_recv()
        total = total + rbuf[off].astype(F32)
    out[...] = out[...] + ens_weight * total

    for which in range(3):
        for off, peer in enumerate(peers):
            small(which, off, peer, me).wait_send()
    for off, peer in enumerate(peers):
        back_copy(off, peer).wait_send()
    for side in range(2):
        static_halo(side).wait_send()

    def drain(c, carry):
        for off, peer in enumerate(peers):
            ens_copy(off, peer, me, c).wait_send()
        for side in range(2):
            halo_copy(side, c).wait_send()
        return carry

    lax.fori_loop(0, pairs, drain, 0)


def covariance(field, ens, sdev, lon_taper, static_taper, loc_vert, static_vert, nlev, nlon):
    members, levs, cols, lats = ens.shape
    half = lon_taper.shape[0] // 2
    pairs = members // nlev // 2
    rows = levs * cols
    full = nlev * rows
    edge = nlev * levs * half
    wide = full + 2 * edge
    flat_field = field.reshape(rows, lats)
    flat_sdev = sdev.reshape(rows, lats)
    spart = (flat_sdev * flat_field).astype(BF16)
    lrep = vert_rows(loc_vert, cols, 128)
    srep = vert_rows(static_vert, cols, 128)
    bands = jnp.concatenate([band_rows(lon_taper, cols, 128), band_rows(static_taper, cols, 128)])
    vmem = pl.BlockSpec(memory_space=pltpu.VMEM)
    dma = pltpu.SemaphoreType.DMA
    out = pl.pallas_call(
        functools.partial(main_kernel, (nlev, nlon, levs, cols, half, pairs)),
        out_shape=jax.ShapeDtypeStruct((rows, lats), F32),
        in_specs=[pl.BlockSpec(memory_space=pl.ANY)] + [vmem] * 6,
        out_specs=vmem,
        scratch_shapes=[
            pltpu.VMEM((2 * pairs, full, lats), BF16),
            pltpu.VMEM((pairs, wide, 2 * lats), BF16),
            pltpu.VMEM((2, pairs, edge, 2 * lats), BF16),
            pltpu.VMEM((full, lats), F32),
            pltpu.VMEM((wide, lats), BF16),
            pltpu.VMEM((2, edge, lats), BF16),
            pltpu.VMEM((full, 128), BF16),
            pltpu.VMEM((full, wide), BF16),
            pltpu.VMEM((rows, wide), BF16),
            pltpu.VMEM((128, wide), BF16),
            pltpu.VMEM((2 * cols, wide), F32),
            pltpu.VMEM((full, lats), F32),
            pltpu.VMEM((full, lats), BF16),
            pltpu.VMEM((nlev - 1, rows, lats), BF16),
            dma,
            dma((nlev - 1, pairs)),
            dma((nlev - 1, pairs)),
            dma((2, pairs + 1)),
            dma((2, pairs + 1)),
            dma((3, nlev - 1)),
            dma((3, nlev - 1)),
            dma((nlev - 1,)),
            dma((nlev - 1,)),
        ],
        compiler_params=pltpu.CompilerParams(
            collective_id=0, has_side_effects=True, vmem_limit_bytes=60 * 1024 * 1024
        ),
        name="covariance",
    )(ens.reshape(members, rows, lats), flat_field, flat_sdev, spart, lrep, srep, bands)
    return out.reshape(levs, cols, lats)


def depart_kernel(
    nlev, nlon, part, value, rinv, live, dep, cost, parts, costs, psend, precv, csend, crecv
):
    me = lax.axis_index("lev")
    lon = lax.axis_index("lon")
    levs = [lax.rem(me + off, nlev) for off in range(1, nlev)]
    lons = [lax.rem(lon + off, nlon) for off in range(1, nlon)]
    barrier = pltpu.get_barrier_semaphore()
    for peer in levs:
        pl.semaphore_signal(barrier, inc=1, device_id={"lev": peer}, device_id_type=MESH)
    for peer in lons:
        pl.semaphore_signal(barrier, inc=1, device_id={"lon": peer}, device_id_type=MESH)
    pl.semaphore_wait(barrier, nlev + nlon - 2)

    def part_copy(off, rank):
        return pltpu.make_async_remote_copy(
            src_ref=part,
            dst_ref=parts.at[rank],
            send_sem=psend.at[off],
            recv_sem=precv.at[off],
            device_id={"lev": levs[off]},
            device_id_type=MESH,
        )

    def cost_copy(off, rank):
        return pltpu.make_async_remote_copy(
            src_ref=costs.at[lon],
            dst_ref=costs.at[rank],
            send_sem=csend.at[off],
            recv_sem=crecv.at[off],
            device_id={"lon": lons[off]},
            device_id_type=MESH,
        )

    for off in range(nlev - 1):
        part_copy(off, me).start()
    parts[me] = part[...]
    for off in range(nlev - 1):
        part_copy(off, lax.rem(me + nlev - off - 1, nlev)).wait_recv()
    hx = parts[0]
    for rank in range(1, nlev):
        hx = hx + parts[rank]
    miss = hx - value[...]
    weighted = jnp.where(live[...] >= 0, rinv[...] * miss, 0.0)
    costs[lon] = jnp.sum(weighted * miss, axis=0, keepdims=True) * 0.5 + jnp.zeros((8, 128), F32)
    dep[...] = weighted
    for off in range(nlon - 1):
        cost_copy(off, lon).start()
    for off in range(nlon - 1):
        cost_copy(off, lax.rem(lon + nlon - off - 1, nlon)).wait_recv()
    total = costs[0]
    for rank in range(1, nlon):
        total = total + costs[rank]
    cost[...] = jnp.sum(total[:1], axis=1, keepdims=True)
    for off in range(nlev - 1):
        part_copy(off, me).wait_send()
    for off in range(nlon - 1):
        cost_copy(off, lon).wait_send()


def departures(part, value, rinv, ids, nlev, nlon):
    shape = (part.shape[0] // 128, 128)
    vmem = pl.BlockSpec(memory_space=pltpu.VMEM)
    dma = pltpu.SemaphoreType.DMA
    dep, cost = pl.pallas_call(
        functools.partial(depart_kernel, nlev, nlon),
        out_shape=(jax.ShapeDtypeStruct(shape, F32), jax.ShapeDtypeStruct((1, 1), F32)),
        in_specs=[vmem] * 4,
        out_specs=(vmem, vmem),
        scratch_shapes=[
            pltpu.VMEM((nlev,) + shape, F32),
            pltpu.VMEM((nlon, 8, 128), F32),
            dma((nlev - 1,)),
            dma((nlev - 1,)),
            dma((nlon - 1,)),
            dma((nlon - 1,)),
        ],
        compiler_params=pltpu.CompilerParams(collective_id=1, has_side_effects=True),
        name="departures",
    )(part.reshape(shape), value.reshape(shape), rinv.reshape(shape), ids.reshape(shape))
    return dep.reshape(-1), cost[0, 0]


def body(
    nlev,
    nlon,
    field,
    ens,
    sdev,
    lon_taper,
    static_taper,
    loc_vert,
    static_vert,
    obs_block,
    obs_value,
    obs_rinv,
    obs_horiz,
    obs_vert,
):
    members, lev_rows, lon_cols, lat_rows = ens.shape
    increment = covariance(
        field, ens, sdev, lon_taper, static_taper, loc_vert, static_vert, nlev, nlon
    )
    block_lon = lon_cols // 8
    block_lat = lat_rows // 16
    nblk = block_lon * block_lat
    slots = obs_block.shape[0]
    blocks = (
        increment.reshape(lev_rows, block_lon, 8, block_lat, 16)
        .transpose(0, 1, 3, 2, 4)
        .reshape(lev_rows * nblk, 128)
    )
    live = obs_block >= 0
    local_ids = obs_block - lax.axis_index("lon") * nblk
    safe = jnp.where(live, local_ids, 0)
    selector = ((jnp.arange(nblk)[:, None] == safe[None, :]) & live[None, :]).astype(F32)
    vert = obs_vert.T
    projected = jnp.dot(blocks, obs_horiz.T, precision=lax.Precision.HIGHEST).reshape(
        lev_rows, nblk, slots
    )
    picked = jnp.sum(projected * selector[None], axis=1)
    partial_value = jnp.sum(picked * vert, axis=0)
    dep, obs_cost = departures(partial_value, obs_value, obs_rinv, obs_block, nlev, nlon)
    weights = vert * dep[None, :]
    spread = (weights[:, None, :] * selector[None]).reshape(lev_rows * nblk, slots)
    adj_blocks = jnp.dot(spread, obs_horiz, precision=lax.Precision.HIGHEST)
    adjoint_field = (
        adj_blocks.reshape(lev_rows, block_lon, block_lat, 8, 16)
        .transpose(0, 1, 3, 2, 4)
        .reshape(lev_rows, lon_cols, lat_rows)
    )
    return (increment, adjoint_field, obs_cost)


def solution(mesh):
    return jax.shard_map(
        functools.partial(body, mesh.shape["lev"], mesh.shape["lon"]),
        mesh=mesh,
        in_specs=(
            P("lev", "lon", None),
            P(None, "lev", "lon", None),
            P("lev", "lon", None),
            P(),
            P(),
            P("lev", None),
            P("lev", None),
            P("lon"),
            P("lon"),
            P("lon"),
            P("lon", None),
            P("lon", "lev"),
        ),
        out_specs=(P("lev", "lon", None), P("lev", "lon", None), P()),
        check_vma=False,
    )
```

time: 398 us -> 209 us (0.53)
  Pallas kernels: 0 us -> 189 us
  blocking collectives: 171 us -> 0 us
  waiting for transfers between devices: 117 us -> 0 us
  local copies, waits for them, and re-layouts: 41.5 us -> 7.02 us
  starting transfers between devices: 31.1 us -> 0 us
  matrix products: 23.3 us -> 5.03 us
  other arithmetic: 11.6 us -> 5.08 us
    pallas_call x0 -> x2, Pallas kernels: none -> 189 us  [the longest x1 177 us: covariance(): pl.pallas_call(functools.partial(main_kernel, (nlev, nlon, levs, cols, ha...]
    all_gather x2 -> x0, blocking collectives: 148 us -> none  [the longest x1 135 us: body(): lax.all_gather(loc_vert, 'lev', axis=0, tiled=True)]
    ppermute x4 -> x0, waiting for transfers between devices: 64.5 us -> none  [the longest x2 64.5 us: padded(): lax.ppermute(lax.slice_in_dim(block, block.shape[dim] - width, None, axis...]
    all_to_all x5 -> x0, waiting for transfers between devices: 52.4 us -> none  [the longest x1 46.5 us: body(): lax.all_to_all(ens, 'lev', split_axis=2, concat_axis=1, tiled=True)]
    all_to_all x5 -> x0, starting transfers between devices: 25 us -> none  [the longest x1 5.57 us: body(): lax.all_to_all(ssmooth, 'lev', split_axis=2, concat_axis=1, tiled=True)]
    psum x2 -> x0, blocking collectives: 22.3 us -> none  [the longest x1 12.3 us: body(): obs_cost = lax.psum(0.5 * jnp.sum(dep * miss), 'lon')]
    dot_general x6 -> x0, matrix products: 17.1 us -> none  [the longest x1 10.5 us: body(): jnp.einsum('lm,kmia->klia', full_loc, zcols, preferred_element_type=jnp.f...]
    convert_element_type x3 -> x0, local copies, waits for them, and re-layouts: 15.6 us -> none  [the longest x1 10.2 us: body(): ens_cols = jnp.sum(ecols.astype(jnp.float32) * zvert, axis=0)[None]]
  transfers between devices with their start and end apart: 9 -> 0, of which waited for: 5 -> 0; matrix products, arithmetic and copies ran while one was open for 16% -> 0% of each run, Pallas kernels for 0% -> 0%
where the time goes in v1:
time: 209 us; the launch traced here: 208 us
  Pallas kernels  189 us (90%)
  local copies, waits for them, and re-layouts  7.02 us (3%)
  other arithmetic  5.08 us (2%)
  matrix products  5.03 us (2%)
  between operations  2.52 us (1%)
    pallas_call x1, Pallas kernels, covariance(): pl.pallas_call(functools.partial(main_kernel, (nlev, nlon, levs, cols, ha...  177 us
    pallas_call x1, Pallas kernels, departures(): pl.pallas_call(functools.partial(depart_kernel, nlev, nlon), out_shape=(j...  12.3 us

profile of v1, /device:TPU:0, one launch (start us, length us, event | category | flops | bytes accessed | tf_op | source)
XLA Modules:
  0.0 208.5 jit_solution(7521390894225214366)
XLA Ops:
  0.6 0.7 convert_element_type.31
  1.3 0.7 convert_element_type.33
  2.0 0.1 select_reduce_fusion.1
  2.1 0.6 pad_maximum_fusion.bands
  2.7 0.7 pad.7
  3.4 0.6 broadcast_in_dim.5
  4.0 0.7 pad.8
  4.7 0.6 broadcast_in_dim.6
  5.4 1.6 multiply_convert_fusion.spart
  7.0 176.6 %covariance.1 = f32[288,128]{1,0:T(8,128)} custom-call(bf16[80,288,128]{2,1,0:T(8,128)(2,1)} %bitcast.43, f32[288,128]{1,0:T(8,128)} %bitcast.46, f32[288,128]{1,0:T(8,128)} %bitcast.47, bf16[288,128]{1,0:T(8,128)(2,1)} %multiply_convert_fusion.spart, bf16[288,128]{1,0:T(8,128)(2,1)} %bitcast.49, bf16[288,128]{1,0:T(8,128)(2,1)} %bitcast.50, ...), custom_call_target="tpu_custom_call" | custom-call | tf_op jit(solution)/shard_map/covariance/pallas_call | solution.py:295
  183.5 1.3 reshape_reshape.3
  184.8 0.2 copy.19
  185.0 0.0 copy-start.3
  185.1 0.0 copy-start
  185.1 0.0 copy-start.2
  185.1 0.3 dot_general.12
  185.4 0.3 copy-done.3
  185.8 0.3 copy-done
  186.1 1.2 fusion
  187.3 0.0 copy-done.2
  187.3 0.6 fusion.6
  187.9 12.3 %departures.1 = (f32[8,128]{1,0:T(8,128)}, f32[1,1]{1,0:T(1,128)}) custom-call(f32[8,128]{1,0:T(8,128)} %bitcast.52, f32[8,128]{1,0:T(8,128)} %bitcast.54, f32[8,128]{1,0:T(8,128)} %bitcast.55, s32[8,128]{1,0:T(8,128)} %bitcast.51), custom_call_target="tpu_custom_call" | custom-call | tf_op jit(solution)/shard_map/departures/pallas_call | solution.py:397
  200.2 0.7 bitcast_multiply_fusion
  200.9 0.1 and_convert_fusion
  201.0 0.2 copy.20
  201.2 3.8 %convolution_bitcast_fusion = f32[18,2,8,8,16]{4,3,2,1,0:T(8,128)S(1)} fusion(f32[8,16,1024,1,1]{2,1,0,4,3:T(8,128)S(1)} %bitcast.48, f32[2,8,1024]{2,1,0:T(8,128)S(1)} %and_convert_fusion, f32[18,1024]{1,0:T(8,128)S(1)} %bitcast_multiply_fusion), kind=kOutput, calls=%fused_computation | convolution fusion | flops 453279744 | bytes 811008 | tf_op jit(solution)/shard_map/dot_general | solution.py:458
  205.0 0.0 copy-start.1
  205.0 1.0 reshape.138
  206.0 0.0 copy-done.1
  206.0 0.7 copy.25
  (5 shorter events, 0.0 us)
Async XLA Ops:
  185.0 0.7 copy-start.3
  185.1 1.0 copy-start
  185.1 2.2 %copy-start.2 = (f32[1024,18]{0,1:T(8,128)S(1)}, f32[1024,18]{0,1:T(8,128)}, u32[]{:S(2)}) copy-start(f32[1024,18]{0,1:T(8,128)} %param.23) | copy-start | bytes 221188
  205.0 1.0 copy-start.1

commit v2 on v1

v2 whole, which is shorter than its diff:
```python
import functools

import jax
import jax.numpy as jnp
from jax import lax
from jax.experimental import pallas as pl
from jax.experimental.pallas import tpu as pltpu
from jax.sharding import PartitionSpec as P

ens_weight = 0.8
static_weight = 0.5
MESH = pl.DeviceIdType.MESH
F32 = jnp.float32
BF16 = jnp.bfloat16


def split(values):
    high = values.astype(BF16)
    return high, (values - high.astype(F32)).astype(BF16)


def swap_groups(source, target, count, lats):
    group = lax.broadcasted_iota(jnp.int32, (count, lats), 1) // 16
    for by in range(8):
        rows = jnp.zeros((count, lats), F32)
        for s in range(8):
            line = source[pl.ds(s, count, stride=8)]
            shift = (16 * (s - by)) % lats
            moved = pltpu.roll(line, shift, 1) if shift else line
            rows = jnp.where(group == s, moved, rows)
        target[pl.ds(by, count, stride=8)] = rows


def main_kernel(
    dims,
    ens,
    field,
    sdev,
    taper,
    static_taper,
    loc,
    svert,
    ids,
    value,
    rinv,
    horiz,
    vert,
    out,
    adj,
    cost,
    ebuf,
    zbuf,
    hsend,
    fbuf,
    spart,
    zs,
    ssend,
    lpad,
    spad,
    lg,
    spread,
    w,
    ws,
    pick,
    tband,
    acc,
    accb,
    rbuf,
    hhigh,
    hlow,
    blocks,
    part,
    parts,
    costs,
    own_sem,
    ens_send,
    ens_recv,
    halo_send,
    halo_recv,
    small_send,
    small_recv,
    back_send,
    back_recv,
    part_send,
    part_recv,
    cost_send,
    cost_recv,
):
    nlev, nlon, levs, cols, half, pairs = dims
    rows = levs * cols
    full = nlev * rows
    edge = nlev * levs * half
    wide = full + 2 * edge
    me = lax.axis_index("lev")
    lon = lax.axis_index("lon")
    right, left = lax.rem(lon + 1, nlon), lax.rem(lon + nlon - 1, nlon)
    peers = [lax.rem(me + off, nlev) for off in range(1, nlev)]
    sources = [lax.rem(me + nlev - off, nlev) for off in range(1, nlev)]

    def slot(rank):
        return pl.ds(pl.multiple_of(rank * rows, 16), rows)

    own_copy = pltpu.make_async_copy(
        ens.at[pl.ds(me * 2 * pairs, 2 * pairs)], ebuf.at[:, slot(me)], own_sem
    )
    own_copy.start()
    width = loc.shape[1]
    for matrix, padded in ((loc, lpad), (svert, spad)):
        padded[...] = jnp.zeros_like(padded)
        padded[:levs, :width] = matrix[...]
    spart[...] = (sdev[...] * field[...]).astype(BF16)
    lons = [lax.rem(lon + off, nlon) for off in range(1, nlon)]

    barrier = pltpu.get_barrier_semaphore()
    for peer in peers:
        pl.semaphore_signal(barrier, inc=1, device_id={"lev": peer}, device_id_type=MESH)
    for peer in lons:
        pl.semaphore_signal(barrier, inc=1, device_id={"lon": peer}, device_id_type=MESH)
    pl.semaphore_wait(barrier, nlev + nlon - 2)

    def small(which, off, peer, rank):
        src, dst = ((lpad, lg), (field, fbuf), (spart, zs))[which]
        return pltpu.make_async_remote_copy(
            src_ref=src,
            dst_ref=dst.at[rank] if which == 0 else dst.at[slot(rank)],
            send_sem=small_send.at[which, off],
            recv_sem=small_recv.at[which, off],
            device_id={"lev": peer},
            device_id_type=MESH,
        )

    def ens_copy(off, peer, rank, c):
        return pltpu.make_async_remote_copy(
            src_ref=ens.at[pl.ds(peer * 2 * pairs + 2 * c, 2)],
            dst_ref=ebuf.at[pl.ds(2 * c, 2), slot(rank)],
            send_sem=ens_send.at[off, c],
            recv_sem=ens_recv.at[off, c],
            device_id={"lev": peer},
            device_id_type=MESH,
        )

    def halo_copy(side, c):
        return pltpu.make_async_remote_copy(
            src_ref=hsend.at[side, c],
            dst_ref=zbuf.at[c, pl.ds(full + side * edge, edge)],
            send_sem=halo_send.at[side, c],
            recv_sem=halo_recv.at[side, c],
            device_id={"lon": (right, left)[side]},
            device_id_type=MESH,
        )

    def static_halo(side):
        return pltpu.make_async_remote_copy(
            src_ref=ssend.at[side],
            dst_ref=zs.at[pl.ds(full + side * edge, edge)],
            send_sem=halo_send.at[side, pairs],
            recv_sem=halo_recv.at[side, pairs],
            device_id={"lon": (right, left)[side]},
            device_id_type=MESH,
        )

    def back_copy(off, peer):
        return pltpu.make_async_remote_copy(
            src_ref=accb.at[slot(peer)],
            dst_ref=rbuf.at[off],
            send_sem=back_send.at[off],
            recv_sem=back_recv.at[off],
            device_id={"lev": peer},
            device_id_type=MESH,
        )

    def part_copy(off, peer, rank):
        return pltpu.make_async_remote_copy(
            src_ref=part,
            dst_ref=parts.at[rank],
            send_sem=part_send.at[off],
            recv_sem=part_recv.at[off],
            device_id={"lev": peer},
            device_id_type=MESH,
        )

    def cost_copy(off, rank):
        return pltpu.make_async_remote_copy(
            src_ref=costs.at[lon],
            dst_ref=costs.at[rank],
            send_sem=cost_send.at[off],
            recv_sem=cost_recv.at[off],
            device_id={"lon": lons[off]},
            device_id_type=MESH,
        )

    for which in range(3):
        for off, peer in enumerate(peers):
            small(which, off, peer, me).start()

    def send_chunk(c, carry):
        for off, peer in enumerate(peers):
            ens_copy(off, peer, me, c).start()
        return carry

    lax.fori_loop(0, pairs, send_chunk, 0)

    lg[me] = lpad[...]
    fbuf[slot(me)] = field[...]
    zs[slot(me)] = spart[...]
    acc[...] = jnp.zeros_like(acc)

    lanes = lpad.shape[1]
    col = lax.broadcasted_iota(jnp.int32, (lanes, wide), 1)
    row = lax.broadcasted_iota(jnp.int32, (lanes, wide), 0)
    inner = col < full
    low = col < full + edge
    tail = jnp.where(low, col - full, col - full - edge)
    level = jnp.where(inner, col // cols, tail // half)
    place = jnp.where(
        inner, half + col % cols, jnp.where(low, tail % half, half + cols + tail % half)
    )
    pick[...] = jnp.where(row == level, 1.0, 0.0).astype(BF16)
    spot = place[:cols] - lax.broadcasted_iota(jnp.int32, (cols, wide), 0)
    for which, weights in enumerate((taper, static_taper)):
        tap = weights[...].astype(F32)
        band = jnp.zeros((cols, wide), F32)
        for d in range(tap.shape[1]):
            band = jnp.where(spot == d, tap[:, d : d + 1], band)
        tband[which * cols : (which + 1) * cols] = band

    padrows = lpad.shape[0]

    def expand(dst, which, rank, first):
        def one(q, carry):
            line = spread[pl.ds(rank * padrows + q, 1)]
            at = pl.ds(pl.multiple_of((first + q) * cols, 16), cols)
            dst[at] = (line * tband[which * cols : (which + 1) * cols]).astype(BF16)
            return carry

        lax.fori_loop(0, levs, one, 0)

    spread[:padrows] = jnp.dot(spad[...], pick[...], preferred_element_type=F32)
    expand(ws, 1, 0, 0)
    hhigh[...], hlow[...] = split(horiz[...])

    for off, rank in enumerate(sources):
        small(0, off, peers[off], rank).wait_recv()

    def expand_loc(rank, carry):
        spread[pl.ds(pl.multiple_of(rank * padrows, 8), padrows)] = jnp.dot(
            lg[rank], pick[...], preferred_element_type=F32
        )
        expand(w, 0, rank, rank * levs)
        return carry

    lax.fori_loop(0, nlev, expand_loc, 0)

    for which in (1, 2):
        for off, rank in enumerate(sources):
            small(which, off, peers[off], rank).wait_recv()

    def edges(values):
        lines = values.reshape(nlev * levs, cols, values.shape[1])
        to_right = lines[:, cols - half :].reshape(edge, values.shape[1]).astype(BF16)
        to_left = lines[:, :half].reshape(edge, values.shape[1]).astype(BF16)
        return to_right, to_left

    ssend[0], ssend[1] = edges(zs[:full].astype(F32))
    own_copy.wait()
    for side in range(2):
        static_halo(side).start()

    tile = full // 3 if full % 48 == 0 else full

    def chunk(c, carry):
        @pl.when(c < pairs)
        def _():
            for off, rank in enumerate(sources):
                ens_copy(off, peers[off], rank, c).wait_recv()
            for h in range(2):
                at = slice(h * 128, (h + 1) * 128)
                product = ebuf[2 * c + h].astype(F32) * fbuf[...]
                hsend[0, c, :, at], hsend[1, c, :, at] = edges(product)
                zbuf[c, :full, at] = product.astype(BF16)
            for side in range(2):
                halo_copy(side, c).start()

        @pl.when(c >= 1)
        def _():
            d = c - 1
            for side in range(2):
                halo_copy(side, d).wait_recv()

            def piece(q, inner_carry):
                at = pl.ds(pl.multiple_of(q * tile, 16), tile)
                zv = jnp.dot(w[at], zbuf[d], preferred_element_type=F32)
                acc[at] += (
                    ebuf[2 * d, at].astype(F32) * zv[:, :128]
                    + ebuf[2 * d + 1, at].astype(F32) * zv[:, 128:]
                )
                return inner_carry

            lax.fori_loop(0, full // tile, piece, 0)

        return carry

    lax.fori_loop(0, pairs + 1, chunk, 0)

    accb[...] = acc[...].astype(BF16)
    for side in range(2):
        static_halo(side).wait_recv()
    static = jnp.dot(ws[...], zs[...], preferred_element_type=F32)
    base = static_weight * sdev[...] * static
    out[...] = base
    for off, peer in enumerate(peers):
        back_copy(off, peer).start()
    total = acc[slot(me)]
    for off, peer in enumerate(peers):
        back_copy(off, peer).wait_recv()
        total = total + rbuf[off].astype(F32)
    out[...] = out[...] + ens_weight * total

    count = rows // 8
    lats = out.shape[1]
    nblk = rows // levs
    slots = ids.shape[1]
    contract = (((1,), (1,)), ((), ()))
    local_ids = ids[...] - lon * nblk
    block = lax.broadcasted_iota(jnp.int32, (nblk, slots), 0)
    chosen = (block == local_ids) & (ids[...] >= 0)
    selector = jnp.where(chosen, 1.0, 0.0)
    swap_groups(out, blocks, count, lats)
    high, low_part = split(blocks[...])
    projected = lax.dot_general(high, hhigh[...], contract, preferred_element_type=F32)
    projected += lax.dot_general(low_part, hhigh[...], contract, preferred_element_type=F32)
    projected += lax.dot_general(high, hlow[...], contract, preferred_element_type=F32)
    picked = jnp.sum(projected.reshape(levs, nblk, slots) * selector[None], axis=1)
    mine = jnp.sum(picked * vert[...], axis=0, keepdims=True)
    part[...] = mine
    parts[me] = mine
    for off, peer in enumerate(peers):
        part_copy(off, peer, me).start()
    for off, rank in enumerate(sources):
        part_copy(off, peers[off], rank).wait_recv()
    hx = parts[0]
    for rank in range(1, nlev):
        hx = hx + parts[rank]
    miss = hx - value[...]
    dep = jnp.where(ids[...] >= 0, rinv[...] * miss, 0.0)
    terms = 0.5 * dep * miss
    folded = terms[:, :128]
    for q in range(1, slots // 128):
        folded = folded + terms[:, q * 128 : (q + 1) * 128]
    costs[lon] = folded
    weighted = vert[...] * dep
    spread_obs = (weighted[:, None, :] * selector[None]).reshape(rows, slots)
    high, low_part = split(spread_obs)
    for off in range(nlon - 1):
        cost_copy(off, lon).start()
    sums = jnp.dot(high, hhigh[...], preferred_element_type=F32)
    sums += jnp.dot(low_part, hhigh[...], preferred_element_type=F32)
    sums += jnp.dot(high, hlow[...], preferred_element_type=F32)
    blocks[...] = sums
    swap_groups(blocks, adj, count, lats)
    for off in range(nlon - 1):
        cost_copy(off, lax.rem(lon + nlon - off - 1, nlon)).wait_recv()
    total_cost = costs[0]
    for rank in range(1, nlon):
        total_cost = total_cost + costs[rank]
    cost[...] = jnp.sum(total_cost, axis=1, keepdims=True)
    for off, peer in enumerate(peers):
        part_copy(off, peer, me).wait_send()
    for off in range(nlon - 1):
        cost_copy(off, lon).wait_send()

    for which in range(3):
        for off, peer in enumerate(peers):
            small(which, off, peer, me).wait_send()
    for off, peer in enumerate(peers):
        back_copy(off, peer).wait_send()
    for side in range(2):
        static_halo(side).wait_send()

    def drain(c, carry):
        for off, peer in enumerate(peers):
            ens_copy(off, peer, me, c).wait_send()
        for side in range(2):
            halo_copy(side, c).wait_send()
        return carry

    lax.fori_loop(0, pairs, drain, 0)


def body(
    nlev,
    nlon,
    field,
    ens,
    sdev,
    lon_taper,
    static_taper,
    loc_vert,
    static_vert,
    obs_block,
    obs_value,
    obs_rinv,
    obs_horiz,
    obs_vert,
):
    members, levs, cols, lats = ens.shape
    half = lon_taper.shape[0] // 2
    pairs = members // nlev // 2
    rows = levs * cols
    full = nlev * rows
    edge = nlev * levs * half
    wide = full + 2 * edge
    slots = obs_block.shape[0]
    padrows = -(-levs // 16) * 16
    vmem = pl.BlockSpec(memory_space=pltpu.VMEM)
    dma = pltpu.SemaphoreType.DMA
    increment, adjoint_field, obs_cost = pl.pallas_call(
        functools.partial(main_kernel, (nlev, nlon, levs, cols, half, pairs)),
        out_shape=(
            jax.ShapeDtypeStruct((rows, lats), F32),
            jax.ShapeDtypeStruct((rows, lats), F32),
            jax.ShapeDtypeStruct((1, 1), F32),
        ),
        in_specs=[pl.BlockSpec(memory_space=pl.ANY)] + [vmem] * 11,
        out_specs=(vmem, vmem, vmem),
        scratch_shapes=[
            pltpu.VMEM((2 * pairs, full, lats), BF16),
            pltpu.VMEM((pairs, wide, 2 * lats), BF16),
            pltpu.VMEM((2, pairs, edge, 2 * lats), BF16),
            pltpu.VMEM((full, lats), F32),
            pltpu.VMEM((rows, lats), BF16),
            pltpu.VMEM((wide, lats), BF16),
            pltpu.VMEM((2, edge, lats), BF16),
            pltpu.VMEM((padrows, 128), BF16),
            pltpu.VMEM((padrows, 128), BF16),
            pltpu.VMEM((nlev, padrows, 128), BF16),
            pltpu.VMEM((nlev * padrows, wide), F32),
            pltpu.VMEM((full, wide), BF16),
            pltpu.VMEM((rows, wide), BF16),
            pltpu.VMEM((128, wide), BF16),
            pltpu.VMEM((2 * cols, wide), F32),
            pltpu.VMEM((full, lats), F32),
            pltpu.VMEM((full, lats), BF16),
            pltpu.VMEM((nlev - 1, rows, lats), BF16),
            pltpu.VMEM((slots, lats), BF16),
            pltpu.VMEM((slots, lats), BF16),
            pltpu.VMEM((rows, lats), F32),
            pltpu.VMEM((1, slots), F32),
            pltpu.VMEM((nlev, 1, slots), F32),
            pltpu.VMEM((nlon, 1, 128), F32),
            dma,
            dma((nlev - 1, pairs)),
            dma((nlev - 1, pairs)),
            dma((2, pairs + 1)),
            dma((2, pairs + 1)),
            dma((3, nlev - 1)),
            dma((3, nlev - 1)),
            dma((nlev - 1,)),
            dma((nlev - 1,)),
            dma((nlev - 1,)),
            dma((nlev - 1,)),
            dma((nlon - 1,)),
            dma((nlon - 1,)),
        ],
        compiler_params=pltpu.CompilerParams(
            collective_id=0, has_side_effects=True, vmem_limit_bytes=60 * 1024 * 1024
        ),
        name="covariance",
    )(
        ens.reshape(members, rows, lats),
        field.reshape(rows, lats),
        sdev.reshape(rows, lats),
        lon_taper.reshape(1, -1),
        static_taper.reshape(1, -1),
        loc_vert,
        static_vert,
        obs_block.reshape(1, slots),
        obs_value.reshape(1, slots),
        obs_rinv.reshape(1, slots),
        obs_horiz,
        obs_vert.T,
    )
    shape = (levs, cols, lats)
    return (increment.reshape(shape), adjoint_field.reshape(shape), obs_cost[0, 0])


def solution(mesh):
    return jax.shard_map(
        functools.partial(body, mesh.shape["lev"], mesh.shape["lon"]),
        mesh=mesh,
        in_specs=(
            P("lev", "lon", None),
            P(None, "lev", "lon", None),
            P("lev", "lon", None),
            P(),
            P(),
            P("lev", None),
            P("lev", None),
            P("lon"),
            P("lon"),
            P("lon"),
            P("lon", None),
            P("lon", "lev"),
        ),
        out_specs=(P("lev", "lon", None), P("lev", "lon", None), P()),
        check_vma=False,
    )
```

time: 209 us -> 187 us (0.89)
  Pallas kernels: 189 us -> 182 us
  other arithmetic: 5.08 us -> 0 us
  matrix products: 5.03 us -> 0 us
  local copies, waits for them, and re-layouts: 7.02 us -> 3.16 us
    pallas_call x2 -> x1, Pallas kernels: 189 us -> 182 us  [body(): pl.pallas_call(functools.partial(main_kernel, (nlev, nlon, levs, cols, ha...]
    dot_general x2 -> x0, matrix products: 5.03 us -> none  [the longest x1 3.84 us: body(): adj_blocks = jnp.dot(spread, obs_horiz, precision=lax.Precision.HIGHEST)]
    convert_element_type x5 -> x0, other arithmetic: 3.04 us -> none  [the longest x1 1.63 us: covariance(): spart = (flat_sdev * flat_field).astype(BF16)]
where the time goes in v2:
time: 187 us
  Pallas kernels  182 us (97%)
  local copies, waits for them, and re-layouts  3.16 us (2%)
  between operations  2.46 us (1%)
    pallas_call x1, Pallas kernels, body(): pl.pallas_call(functools.partial(main_kernel, (nlev, nlon, levs, cols, ha...  182 us

profile of v2, /device:TPU:0, one launch (start us, length us, event | category | flops | bytes accessed | tf_op | source)
XLA Modules:
  0.0 187.3 jit_solution(2078642974360676885)
XLA Ops:
  0.6 181.7 %covariance.1 = (f32[288,128]{1,0:T(8,128)}, f32[288,128]{1,0:T(8,128)}, f32[1,1]{1,0:T(1,128)}) custom-call(bf16[80,288,128]{2,1,0:T(8,128)(2,1)} %bitcast.12, f32[288,128]{1,0:T(8,128)} %bitcast.13, f32[288,128]{1,0:T(8,128)} %bitcast.14, bf16[1,17]{1,0:T(2,128)(2,1)} %bitcast.21, bf16[1,17]{1,0:T(2,128)(2,1)} %bitcast.22, bf16[18,72]{1,0:T(8,128)(2,1)} %loc.1, ...), custom_call_target="tpu_custom_call" | custom-call | tf_op jit(solution)/shard_map/covariance/pallas_call | solution.py:417
  182.3 1.6 copy.18
  183.9 1.6 copy.19

commit v3 on v2

--- a/solution.py
+++ b/solution.py
@@ -131,20 +131,21 @@
 
     def ens_copy(off, peer, rank, c):
         return pltpu.make_async_remote_copy(
-            src_ref=ens.at[pl.ds(peer * 2 * pairs + 2 * c, 2)],
-            dst_ref=ebuf.at[pl.ds(2 * c, 2), slot(rank)],
+            src_ref=ens.at[peer * 2 * pairs + c],
+            dst_ref=ebuf.at[c, slot(rank)],
             send_sem=ens_send.at[off, c],
             recv_sem=ens_recv.at[off, c],
             device_id={"lev": peer},
             device_id_type=MESH,
         )
 
-    def halo_copy(side, c):
-        return pltpu.make_async_remote_copy(
-            src_ref=hsend.at[side, c],
-            dst_ref=zbuf.at[c, pl.ds(full + side * edge, edge)],
-            send_sem=halo_send.at[side, c],
-            recv_sem=halo_recv.at[side, c],
+    def halo_copy(side, c, h):
+        at = pl.ds(h * 128, 128)
+        return pltpu.make_async_remote_copy(
+            src_ref=hsend.at[side, c, :, at],
+            dst_ref=zbuf.at[c, pl.ds(full + side * edge, edge), at],
+            send_sem=halo_send.at[side, 2 * c + h],
+            recv_sem=halo_recv.at[side, 2 * c + h],
             device_id={"lon": (right, left)[side]},
             device_id_type=MESH,
         )
@@ -153,8 +154,8 @@
         return pltpu.make_async_remote_copy(
             src_ref=ssend.at[side],
             dst_ref=zs.at[pl.ds(full + side * edge, edge)],
-            send_sem=halo_send.at[side, pairs],
-            recv_sem=halo_recv.at[side, pairs],
+            send_sem=halo_send.at[side, 2 * pairs],
+            recv_sem=halo_recv.at[side, 2 * pairs],
             device_id={"lon": (right, left)[side]},
             device_id_type=MESH,
         )
@@ -189,7 +190,7 @@
             device_id_type=MESH,
         )
 
-    for which in range(3):
+    for which in range(2):
         for off, peer in enumerate(peers):
             small(which, off, peer, me).start()
 
@@ -198,7 +199,9 @@
             ens_copy(off, peer, me, c).start()
         return carry
 
-    lax.fori_loop(0, pairs, send_chunk, 0)
+    lax.fori_loop(0, 2 * pairs, send_chunk, 0)
+    for off, peer in enumerate(peers):
+        small(2, off, peer, me).start()
 
     lg[me] = lpad[...]
     fbuf[slot(me)] = field[...]
@@ -251,9 +254,8 @@
 
     lax.fori_loop(0, nlev, expand_loc, 0)
 
-    for which in (1, 2):
-        for off, rank in enumerate(sources):
-            small(which, off, peers[off], rank).wait_recv()
+    for off, rank in enumerate(sources):
+        small(1, off, peers[off], rank).wait_recv()
 
     def edges(values):
         lines = values.reshape(nlev * levs, cols, values.shape[1])
@@ -261,31 +263,37 @@
         to_left = lines[:, :half].reshape(edge, values.shape[1]).astype(BF16)
         return to_right, to_left
 
-    ssend[0], ssend[1] = edges(zs[:full].astype(F32))
     own_copy.wait()
-    for side in range(2):
-        static_halo(side).start()
 
     tile = full // 3 if full % 48 == 0 else full
 
     def chunk(c, carry):
         @pl.when(c < pairs)
         def _():
-            for off, rank in enumerate(sources):
-                ens_copy(off, peers[off], rank, c).wait_recv()
             for h in range(2):
+                for off, rank in enumerate(sources):
+                    ens_copy(off, peers[off], rank, 2 * c + h).wait_recv()
                 at = slice(h * 128, (h + 1) * 128)
                 product = ebuf[2 * c + h].astype(F32) * fbuf[...]
                 hsend[0, c, :, at], hsend[1, c, :, at] = edges(product)
                 zbuf[c, :full, at] = product.astype(BF16)
+                for side in range(2):
+                    halo_copy(side, c, h).start()
+
+        @pl.when(c == pairs)
+        def _():
+            for off, rank in enumerate(sources):
+                small(2, off, peers[off], rank).wait_recv()
+            ssend[0], ssend[1] = edges(zs[:full].astype(F32))
             for side in range(2):
-                halo_copy(side, c).start()
+                static_halo(side).start()
 
         @pl.when(c >= 1)
         def _():
             d = c - 1
-            for side in range(2):
-                halo_copy(side, d).wait_recv()
+            for h in range(2):
+                for side in range(2):
+                    halo_copy(side, d, h).wait_recv()
 
             def piece(q, inner_carry):
                 at = pl.ds(pl.multiple_of(q * tile, 16), tile)
@@ -378,10 +386,11 @@
         static_halo(side).wait_send()
 
     def drain(c, carry):
-        for off, peer in enumerate(peers):
-            ens_copy(off, peer, me, c).wait_send()
-        for side in range(2):
-            halo_copy(side, c).wait_send()
+        for h in range(2):
+            for off, peer in enumerate(peers):
+                ens_copy(off, peer, me, 2 * c + h).wait_send()
+            for side in range(2):
+                halo_copy(side, c, h).wait_send()
         return carry
 
     lax.fori_loop(0, pairs, drain, 0)
@@ -449,10 +458,10 @@
             pltpu.VMEM((nlev, 1, slots), F32),
             pltpu.VMEM((nlon, 1, 128), F32),
             dma,
-            dma((nlev - 1, pairs)),
-            dma((nlev - 1, pairs)),
-            dma((2, pairs + 1)),
-            dma((2, pairs + 1)),
+            dma((nlev - 1, 2 * pairs)),
+            dma((nlev - 1, 2 * pairs)),
+            dma((2, 2 * pairs + 1)),
+            dma((2, 2 * pairs + 1)),
             dma((3, nlev - 1)),
             dma((3, nlev - 1)),
             dma((nlev - 1,)),

time: 187 us -> 184 us (0.984)
  Pallas kernels: 182 us -> 179 us
    pallas_call x1, Pallas kernels: 182 us -> 179 us  [body(): pl.pallas_call(functools.partial(main_kernel, (nlev, nlon, levs, cols, ha...]
where the time goes in v3:
time: 184 us
  Pallas kernels  179 us (97%)
  local copies, waits for them, and re-layouts  3.16 us (2%)
  between operations  2.46 us (1%)
    pallas_call x1, Pallas kernels, body(): pl.pallas_call(functools.partial(main_kernel, (nlev, nlon, levs, cols, ha...  179 us

profile of v3, /device:TPU:0, one launch (start us, length us, event | category | flops | bytes accessed | tf_op | source)
XLA Modules:
  0.0 184.3 jit_solution(1148757204537434068)
XLA Ops:
  0.6 178.6 %covariance.1 = (f32[288,128]{1,0:T(8,128)}, f32[288,128]{1,0:T(8,128)}, f32[1,1]{1,0:T(1,128)}) custom-call(bf16[80,288,128]{2,1,0:T(8,128)(2,1)} %bitcast.12, f32[288,128]{1,0:T(8,128)} %bitcast.13, f32[288,128]{1,0:T(8,128)} %bitcast.14, bf16[1,17]{1,0:T(2,128)(2,1)} %bitcast.21, bf16[1,17]{1,0:T(2,128)(2,1)} %bitcast.22, bf16[18,72]{1,0:T(8,128)(2,1)} %loc.1, ...), custom_call_target="tpu_custom_call" | custom-call | tf_op jit(solution)/shard_map/covariance/pallas_call | solution.py:426
  179.3 1.6 copy.18
  180.9 1.6 copy.19
